TPU v7x, 32 devices: a whole 2x2x4 slice. The times are simulated.
32 devices in a mesh: gx: 4 (over z), gy: 8 (over y, x, core).
Axes of the slice: x: 2, y: 2, z: 4, core: 2. Of those that a mesh axis runs over, the one named last changes fastest.
Arguments:
- state_prev: float32 [128, 128, 512], P('gy', None, 'gx'), may hold values from -60 to 60
- diffusivity: float32 [128, 128, 512], P('gy', None, 'gx'), may hold values from 0.5 to 4
- vapour: float32 [128, 128, 512], P('gy', None, 'gx'), may hold values from 0.01 to 0.1
- cos_zenith: float32 [128, 512], P('gy', 'gx'), may hold values from 0.1 to 1
- albedo: float32 [128, 512], P('gy', 'gx'), may hold values from 0.05 to 0.8
- absorption: float32 [128, 112], replicated, may hold values from 0.005 to 1
- solar_weight: float32 [112], replicated, may hold values from 0.002 to 0.02
- day_mask: int32 [512], P(('gx', 'gy')), may hold values from 0 to 1, as said below
Outputs:
- state_next: float32 [128, 128, 512], P('gy', None, 'gx')
- residual: float32 [128, 128, 512], P('gy', None, 'gx')
- net_flux: float32 [128, 128, 512], P('gy', None, 'gx')
Inputs may be any that keep to these rules, and one draw needn't show every extreme that they name: `day_mask`: exactly half of the 512 entries are 1, and some device holds only sunlit blocks.
All inputs are finite; a program needn't handle non-finite values.
Results may differ from a plain program's by a relative error of at most 0.00015.
Values sent between devices are 32-bit elements; how exact they have to be, the bound alone decides.
A program may use at most 128 MiB of HBM per device.

v0:
```python
import functools
import math

import jax
import jax.numpy as jnp
from jax import lax
from jax.experimental import pallas as pl
from jax.experimental.pallas import tpu as pltpu
from jax.sharding import PartitionSpec as P

ITERS = 5
SUB = 8
WINDOWS = ITERS + 3
UNROLL = 32
LOG2E = math.log2(math.e)
MESH = pl.DeviceIdType.MESH
F32 = jnp.float32


def edge(rows, w):
    return max(0, rows * (2 * w - 1) // (2 * WINDOWS))


def radiate(j, state, vapour_ref, cos_ref, albedo_ref, maskv_ref, wcol_ref, wide, scales, partial, net_ref):
    levels, gpoints, lanes = wide.shape
    down_scale, up_scale = scales.at[0], scales.at[1]
    cosine = cos_ref[pl.ds(j, 1), :]
    optical = vapour_ref[j] * (1.0 + 0.5 * jnp.tanh(state))
    down_scale[...] = optical * (-LOG2E / cosine)
    up_scale[...] = optical * (-1.66 * LOG2E)

    def downward(l, carry):
        carry = carry * jnp.exp2(wide[l] * down_scale[pl.ds(l, 1), :])
        partial[pl.ds(pl.multiple_of(l * SUB, SUB), SUB), :] = jnp.sum(
            carry.reshape(gpoints // SUB, SUB, lanes), 0
        )
        return carry

    carry = lax.fori_loop(0, levels, downward, wcol_ref[...] * cosine, unroll=UNROLL)
    carry = carry * albedo_ref[pl.ds(j, 1), :]

    def upward(i, carry):
        l = levels - 1 - i
        where = pl.ds(pl.multiple_of(l * SUB, SUB), SUB)
        partial[where, :] = partial[where, :] - jnp.sum(
            carry.reshape(gpoints // SUB, SUB, lanes), 0
        )
        return carry * jnp.exp2(wide[l] * up_scale[pl.ds(l, 1), :])

    lax.fori_loop(0, levels, upward, carry, unroll=UNROLL)
    total = partial[pl.ds(0, levels, stride=SUB), :]
    for s in range(1, SUB):
        total = total + partial[pl.ds(s, levels, stride=SUB), :]
    net_ref[j] = total * maskv_ref[pl.ds(j, 1), :]


def solve_kernel(
    nx, ny,
    state_hbm, diff_hbm, vapour_hbm, cos_hbm, albedo_hbm, mask_hbm, absorb_hbm, weight_hbm,
    basis, xs, ds, vapour_ref, cos_ref, albedo_ref, net_ref, wide, wcol, maskv, coef,
    root, degree, gain_d, inverse_d, absorb, weight_row, mask_smem,
    lon_send, lon_recv, lon_halo, scales, partial, sums, mine, stage_one, half_sum, stage_two,
    in_sem, lat_ssem, lat_rsem, lon_ssem, lon_rsem, one_ssem, one_rsem, two_ssem, two_rsem,
):
    rows, levels, lanes = vapour_ref.shape
    gpoints = wide.shape[1]
    tiles = levels // SUB
    per = lanes // (2 * tiles)
    groups = rows // per
    moments = 2 * ITERS + 1
    ix = lax.axis_index("gx")
    iy = lax.axis_index("gy")
    gx_east, gx_west = lax.rem(ix + 1, nx), lax.rem(ix + nx - 1, nx)
    inside = pl.ds(1, rows)

    loads = [
        pltpu.make_async_copy(src, dst, in_sem.at[i])
        for i, (src, dst) in enumerate([
            (diff_hbm, ds.at[inside]), (state_hbm, xs.at[inside]), (absorb_hbm, absorb),
            (weight_hbm, weight_row), (mask_hbm, mask_smem), (cos_hbm, cos_ref),
            (albedo_hbm, albedo_ref), (vapour_hbm, vapour_ref),
        ])
    ]
    for load in loads:
        load.start()

    barrier = pltpu.get_barrier_semaphore()
    for d in range(1, nx):
        pl.semaphore_signal(
            barrier, inc=1, device_id=(lax.rem(ix + d, nx), iy), device_id_type=MESH
        )
    for d in range(1, ny):
        pl.semaphore_signal(
            barrier, inc=1, device_id=(ix, lax.rem(iy + d, ny)), device_id_type=MESH
        )

    lane = lax.broadcasted_iota(jnp.int32, (SUB, lanes), 1)
    sub = lax.broadcasted_iota(jnp.int32, (SUB, lanes), 0)
    first_lane, last_lane = lane == 0, lane == lanes - 1
    first_sub, last_sub = sub == 0, sub == SUB - 1
    even_lane = (lane & 1) == 0
    zero = jnp.zeros((SUB, lanes), F32)

    def field(k):
        return ds if k == 0 else xs if k == 1 else basis.at[k - 2]

    def lat_copy(k, side):
        ref = field(k) if isinstance(k, int) else basis.at[k - 2]
        return pltpu.make_async_remote_copy(
            src_ref=ref.at[1 if side == 0 else rows],
            dst_ref=ref.at[rows + 1 if side == 0 else 0],
            send_sem=lat_ssem.at[k, side],
            recv_sem=lat_rsem.at[k, side],
            device_id=(ix, lax.rem(iy + ny - 1, ny) if side == 0 else lax.rem(iy + 1, ny)),
            device_id_type=MESH,
        )

    def lon_copy(k, side):
        return pltpu.make_async_remote_copy(
            src_ref=lon_send.at[k],
            dst_ref=lon_recv.at[k, side],
            send_sem=lon_ssem.at[k, side],
            recv_sem=lon_rsem.at[k, side],
            device_id=(gx_west if side == 0 else gx_east, iy),
            device_id_type=MESH,
        )

    def send_halo(k):
        @pl.when(iy > 0)
        def _():
            lat_copy(k, 0).start()

        @pl.when(iy < ny - 1)
        def _():
            lat_copy(k, 1).start()

        for side in range(2):
            lon_copy(k, side).start()

    def wait_halo(k):
        @pl.when(iy > 0)
        def _():
            lat_copy(k, 0).wait_send()
            lat_copy(k, 1).wait_recv()

        @pl.when(iy < ny - 1)
        def _():
            lat_copy(k, 1).wait_send()
            lat_copy(k, 0).wait_recv()

        for side in range(2):
            lon_copy(k, side).wait()

    def merged(k, g):
        west = lon_recv[k, 1, g * SUB:(g + 1) * SUB, :]
        east = pltpu.roll(lon_recv[k, 0, g * SUB:(g + 1) * SUB, :], lanes - 2, 1)
        return jnp.where(even_lane, west, east)

    bits = [((lane >> (1 + b)) & 1) == 1 for b in range((lanes // 2 - 1).bit_length())]

    def pack(pieces):
        level = [pltpu.roll(piece, (2 * q + 1) % lanes, 1) for q, piece in enumerate(pieces)]
        for mask in bits:
            level = [jnp.where(mask, b, a) for a, b in zip(level[::2], level[1::2])]
        return level[0]

    def group_rows(g):
        return pl.ds(pl.multiple_of(g * SUB, SUB), SUB)

    def lon_pair(value, halo, q):
        moved = pltpu.roll(halo, (lanes - 2 * q) % lanes, 1)
        return (
            jnp.where(last_lane, moved, pltpu.roll(value, lanes - 1, 1)),
            jnp.where(first_lane, moved, pltpu.roll(value, 1, 1)),
        )

    def vertical_pair(values):
        later = [pltpu.roll(v, 1, 0) for v in values]
        sooner = [pltpu.roll(v, SUB - 1, 0) for v in values]
        above = [jnp.where(first_sub, later[t - 1] if t else zero, later[t]) for t in range(tiles)]
        below = [
            jnp.where(last_sub, sooner[t + 1] if t < tiles - 1 else zero, sooner[t])
            for t in range(tiles)
        ]
        return above, below

    def plane_of(ref, j):
        return [ref[j, t * SUB:(t + 1) * SUB, :] for t in range(tiles)]

    def reduce_copy(r, stage, d):
        buffer = stage_one if stage == 0 else stage_two
        slot = ix if stage == 0 else iy
        ssem = one_ssem if stage == 0 else two_ssem
        rsem = one_rsem if stage == 0 else two_rsem
        peer = (lax.rem(ix + d, nx), iy) if stage == 0 else (ix, lax.rem(iy + d, ny))
        return pltpu.make_async_remote_copy(
            src_ref=(mine if stage == 0 else half_sum).at[r],
            dst_ref=buffer.at[r, slot],
            send_sem=ssem.at[r, d - 1],
            recv_sem=rsem.at[r, d - 1],
            device_id=peer,
            device_id_type=MESH,
        )

    def reduce_start(r, stage):
        source, buffer = (mine, stage_one) if stage == 0 else (half_sum, stage_two)
        n = nx if stage == 0 else ny
        buffer[r, ix if stage == 0 else iy] = source[r]
        for d in range(1, n):
            reduce_copy(r, stage, d).start()

    def reduce_end(r, stage):
        n = nx if stage == 0 else ny
        for d in range(1, n):
            reduce_copy(r, stage, d).wait()
        buffer = stage_one if stage == 0 else stage_two
        total = buffer[r, 0]
        for d in range(1, n):
            total = total + buffer[r, d]
        return total

    def all_lanes(values):
        shift = lanes // 2
        while shift:
            values = values + pltpu.roll(values, shift, 1)
            shift //= 2
        return values

    def window(first, last):
        @pl.loop(first, last)
        def _(j):
            radiate(
                j, xs[j + 1], vapour_ref, cos_ref, albedo_ref, maskv, wcol, wide, scales,
                partial, net_ref,
            )

    for k in range(2, 2 + ITERS):
        @pl.when(iy == 0)
        def _():
            basis[k - 2, 0] = jnp.zeros((levels, lanes), F32)

        @pl.when(iy == ny - 1)
        def _():
            basis[k - 2, rows + 1] = jnp.zeros((levels, lanes), F32)

    for k in range(2):
        loads[k].wait()
        if k == 0:
            pl.semaphore_wait(barrier, nx + ny - 2)

        @pl.loop(0, groups)
        def _(g):
            pieces = []
            for i in range(per):
                pieces += plane_of(field(k), g * per + i + 1)
            lon_send[k, group_rows(g), :] = pack(pieces)

        send_halo(k)

    def spread(j, total):
        part = zero
        for t in range(tiles):
            here = pl.ds(t * SUB, SUB)
            d = ds[j + 1, here, :]
            reciprocal = lax.rsqrt(d)
            root[j + 1, here, :] = d * reciprocal
            inverse_d[j, here, :] = reciprocal * reciprocal
            square = d * d
            part = part + square * square * square
        return total + part

    squares = lax.fori_loop(0, rows, spread, zero)
    mine[0] = jnp.concatenate([squares, jnp.zeros_like(squares)], 0)
    reduce_start(0, 0)

    for load in loads[2:]:
        load.wait()

    for j in range(rows):
        maskv[j:j + 1, :] = jnp.full((1, lanes), mask_smem[j].astype(F32), F32)
    column = jnp.broadcast_to(weight_row[...], (lanes, gpoints)).T
    wcol[...] = column

    spans = 4

    @pl.loop(0, spans)
    def _(i):
        span = levels // spans
        turned = pltpu.roll(absorb[...], lax.rem(levels - i * span, levels), 1)
        for m in range(span):
            wide[i * span + m] = jnp.broadcast_to(turned[:, m:m + 1], (gpoints, lanes))

    window(0, edge(rows, 1))
    half_sum[0] = reduce_end(0, 0)
    reduce_start(0, 1)

    wait_halo(0)
    wait_halo(1)

    @pl.when(iy > 0)
    def _():
        root[0] = ds[0] * lax.rsqrt(ds[0])

    @pl.when(iy == 0)
    def _():
        root[0] = jnp.zeros((levels, lanes), F32)
        xs[0] = jnp.zeros((levels, lanes), F32)

    @pl.when(iy < ny - 1)
    def _():
        root[rows + 1] = ds[rows + 1] * lax.rsqrt(ds[rows + 1])

    @pl.when(iy == ny - 1)
    def _():
        root[rows + 1] = jnp.zeros((levels, lanes), F32)
        xs[rows + 1] = jnp.zeros((levels, lanes), F32)

    for g in range(groups):
        d = merged(0, g)
        lon_halo[0, g * SUB:(g + 1) * SUB, :] = d * lax.rsqrt(d)
        lon_halo[1, g * SUB:(g + 1) * SUB, :] = merged(1, g)

    @pl.loop(0, groups)
    def _(g):
        root_halo = lon_halo[0, group_rows(g), :]
        x_halo = lon_halo[1, group_rows(g), :]
        pieces = []
        for i in range(per):
            j = g * per + i
            s_here, x_here = plane_of(root, j + 1), plane_of(xs, j + 1)
            s_above, s_below = vertical_pair(s_here)
            x_above, x_below = vertical_pair(x_here)
            for t in range(tiles):
                at = pl.ds(t * SUB, SUB)
                q = i * tiles + t
                s_pairs = lon_pair(s_here[t], root_halo, q) + (
                    root[j + 2, at, :], root[j, at, :], s_above[t], s_below[t]
                )
                x_pairs = lon_pair(x_here[t], x_halo, q) + (
                    xs[j + 2, at, :], xs[j, at, :], x_above[t], x_below[t]
                )
                around, change = None, None
                for s, x in zip(s_pairs, x_pairs):
                    term = s * (x - x_here[t])
                    around = s if around is None else around + s
                    change = term if change is None else change + term
                degree[j, at, :] = s_here[t] * around
                start = ds[j + 1, at, :] * change
                basis[0, j + 1, at, :] = start
                pieces.append(start)
        lon_send[2, group_rows(g), :] = pack(pieces)

    send_halo(2)
    window(edge(rows, 1), edge(rows, 2))
    squares = reduce_end(0, 1)
    count = nx * ny * rows * levels * lanes
    squares = all_lanes(jnp.sum(squares, 0, keepdims=True))
    half = 6.0 * jnp.exp(jnp.log(squares * (1.0 / count)) * (1.0 / 6.0))
    twice = jnp.broadcast_to(2.0 / half, (SUB, lanes))

    def advance(k, first, last):
        wait_halo(2 + k)
        for g in range(groups):
            lon_halo[0, g * SUB:(g + 1) * SUB, :] = merged(2 + k, g)
        here, there = basis.at[k], basis.at[k + 1]

        def step(g, totals):
            halo = lon_halo[0, group_rows(g), :]
            pieces = []
            parts = [zero] * len(totals)
            for i in range(per):
                j = g * per + i
                u = plane_of(here, j + 1)
                above, below = vertical_pair(u)
                for t in range(tiles):
                    at = pl.ds(t * SUB, SUB)
                    east, west = lon_pair(u[t], halo, i * tiles + t)
                    around = ((east + west) + (above[t] + below[t])) + (
                        here[j + 2, at, :] + here[j, at, :]
                    )
                    if first:
                        own = twice * degree[j, at, :] - 2.0
                        other = twice * ds[j + 1, at, :]
                        degree[j, at, :] = own
                        gain_d[j, at, :] = other
                        later = 0.5 * (own * u[t] - other * around)
                    else:
                        later = degree[j, at, :] * u[t] - gain_d[j, at, :] * around
                        later = later - basis[k - 1, j + 1, at, :]
                    there[j + 1, at, :] = later
                    weighed = later * inverse_d[j, at, :]
                    parts[0] = parts[0] + weighed * u[t]
                    parts[1] = parts[1] + weighed * later
                    if first:
                        parts[2] = parts[2] + (u[t] * inverse_d[j, at, :]) * u[t]
                    pieces.append(later)
            if not last:
                lon_send[3 + k, group_rows(g), :] = pack(pieces)
            return tuple(a + b for a, b in zip(totals, parts))

        totals = lax.fori_loop(0, groups, step, (zero,) * (3 if first else 2))
        sums[2 * k + 1] = totals[0]
        sums[2 * k + 2] = totals[1]
        if first:
            sums[0] = totals[2]

    for k in range(ITERS):
        advance(k, k == 0, k == ITERS - 1)
        if k < ITERS - 1:
            send_halo(3 + k)
            window(edge(rows, 2 + k), edge(rows, 3 + k))

    lines = [jnp.sum(sums[m], 0, keepdims=True) for m in range(moments)]
    lines += [jnp.zeros_like(lines[0])] * (2 * SUB - moments)
    mine[1] = jnp.concatenate(lines, 0)
    reduce_start(1, 0)
    window(edge(rows, ITERS + 1), edge(rows, ITERS + 2))
    half_sum[1] = reduce_end(1, 0)
    reduce_start(1, 1)
    window(edge(rows, ITERS + 2), edge(rows, ITERS + 3))
    values = all_lanes(reduce_end(1, 1))
    raw = [values[m:m + 1, :] for m in range(moments)]

    mu = [raw[0], raw[1]]
    for k in range(1, ITERS + 1):
        mu.append(2.0 * raw[2 * k] - mu[0])
        if k < ITERS:
            mu.append(2.0 * raw[2 * k + 1] - mu[1])
    gram = [
        [0.5 * (mu[i + j] + mu[abs(i - j)]) for j in range(ITERS + 1)] for i in range(ITERS + 1)
    ]

    def inner(a, b):
        terms = []
        for i in range(len(a)):
            for j in range(len(b)):
                terms.append((a[i] * b[j]) * gram[i][j])
        while len(terms) > 1:
            terms = [
                terms[i] + terms[i + 1] if i + 1 < len(terms) else terms[i]
                for i in range(0, len(terms), 2)
            ]
        return terms[0]

    centre = half + 1.0
    one = jnp.ones_like(half)
    none = jnp.zeros_like(half)
    res, direction, gain = [one], [one], [none] * ITERS
    current = inner(res, res)
    for iteration in range(ITERS):
        image = [centre * c for c in direction] + [none]
        for j, c in enumerate(direction):
            if j == 0:
                image[1] = image[1] + half * c
            else:
                image[j + 1] = image[j + 1] + 0.5 * half * c
                image[j - 1] = image[j - 1] + 0.5 * half * c
        step = current / inner(direction, image)
        for j, c in enumerate(direction):
            gain[j] = gain[j] + step * c
        res = [r - step * q for r, q in zip(res + [none], image)]
        if iteration < ITERS - 1:
            following = inner(res, res)
            ratio = following / current
            direction = [r + ratio * c for r, c in zip(res, direction + [none])]
            current = following

    lines = gain + res
    lines += [none] * (2 * SUB - len(lines))
    coef[...] = jnp.concatenate(lines, 0)


def finish_kernel(
    basis, xs, ds, vapour_ref, cos_ref, albedo_ref, net_ref, wide, wcol, maskv, coef,
    next_hbm, residual_hbm, net_hbm,
    next_ref, residual_ref, rest, scales, partial, sems,
):
    rows, levels, lanes = vapour_ref.shape
    tiles = levels // SUB
    done = edge(rows, WINDOWS)
    chunk = rows // 4
    early = pltpu.make_async_copy(
        net_ref.at[pl.ds(0, done)], net_hbm.at[pl.ds(0, done)], sems.at[0, 0]
    )
    early.start()
    lines = [
        jnp.broadcast_to(coef[m:m + 1, :], (SUB, lanes)) for m in range(2 * ITERS + 1)
    ]
    gain, res = lines[:ITERS], lines[ITERS:]
    copies = []
    for c in range(rows // chunk):
        @pl.loop(c * chunk, (c + 1) * chunk)
        def _(j):
            for t in range(tiles):
                at = pl.ds(t * SUB, SUB)
                base = [basis[k, j + 1, at, :] for k in range(ITERS + 1)]
                scale = lax.rsqrt(ds[j + 1, at, :])
                moved, left = gain[0] * base[0], res[0] * base[0]
                for k in range(1, ITERS + 1):
                    if k < ITERS:
                        moved = moved + gain[k] * base[k]
                    left = left + res[k] * base[k]
                next_ref[j, at, :] = xs[j + 1, at, :] + scale * moved
                residual_ref[j, at, :] = scale * left

        part = pl.ds(c * chunk, chunk)
        for i, (source, target) in enumerate([(next_ref, next_hbm), (residual_ref, residual_hbm)]):
            copies.append(pltpu.make_async_copy(source.at[part], target.at[part], sems.at[1 + i, c]))
            copies[-1].start()

    for j in range(done, rows):
        radiate(
            j, xs[j + 1], vapour_ref, cos_ref, albedo_ref, maskv, wcol, wide, scales,
            partial, rest,
        )
    late = pltpu.make_async_copy(
        rest.at[pl.ds(done, rows - done)], net_hbm.at[pl.ds(done, rows - done)], sems.at[0, 1]
    )
    late.start()
    for copy in [early] + copies + [late]:
        copy.wait()


def body(mesh_shape, state_prev, diffusivity, vapour, cos_zenith, albedo, absorption, solar_weight, day_mask):
    nx, ny = mesh_shape
    rows, levels, lanes = state_prev.shape
    gpoints = absorption.shape[1]
    weight = solar_weight[None, :]
    absorb = absorption.T
    vmem = pl.BlockSpec(memory_space=pltpu.VMEM)
    hbm = pl.BlockSpec(memory_space=pltpu.HBM)
    dma = pltpu.SemaphoreType.DMA
    kinds = ITERS + 2
    packs = 2 * rows * (levels // SUB) // lanes * SUB
    cells = (rows, levels, lanes)
    around = (rows + 2, levels, lanes)
    scales = pltpu.VMEM((2, levels, lanes), F32)
    partial = pltpu.VMEM((levels * SUB, lanes), F32)
    held = pl.pallas_call(
        functools.partial(solve_kernel, nx, ny),
        out_shape=[
            pltpu.VMEM((ITERS + 1,) + around, F32),
            pltpu.VMEM(around, F32),
            pltpu.VMEM(around, F32),
            pltpu.VMEM(cells, F32),
            pltpu.VMEM((rows, lanes), F32),
            pltpu.VMEM((rows, lanes), F32),
            pltpu.VMEM(cells, F32),
            pltpu.VMEM((levels, gpoints, lanes), F32),
            pltpu.VMEM((gpoints, lanes), F32),
            pltpu.VMEM((rows, lanes), F32),
            pltpu.VMEM((2 * SUB, lanes), F32),
        ],
        in_specs=[hbm] * 8,
        out_specs=[vmem] * 11,
        scratch_shapes=[
            pltpu.VMEM(around, F32),
            pltpu.VMEM(cells, F32),
            pltpu.VMEM(cells, F32),
            pltpu.VMEM(cells, F32),
            pltpu.VMEM((gpoints, levels), F32),
            pltpu.VMEM((1, gpoints), F32),
            pltpu.SMEM((rows,), jnp.int32),
            pltpu.VMEM((kinds, packs, lanes), F32),
            pltpu.VMEM((kinds, 2, packs, lanes), F32),
            pltpu.VMEM((2, packs, lanes), F32),
            scales,
            partial,
            pltpu.VMEM((2 * ITERS + 1, SUB, lanes), F32),
            pltpu.VMEM((2, 2 * SUB, lanes), F32),
            pltpu.VMEM((2, nx, 2 * SUB, lanes), F32),
            pltpu.VMEM((2, 2 * SUB, lanes), F32),
            pltpu.VMEM((2, ny, 2 * SUB, lanes), F32),
            dma((8,)),
            dma((kinds, 2)), dma((kinds, 2)), dma((kinds, 2)), dma((kinds, 2)),
            dma((2, nx)), dma((2, nx)), dma((2, ny)), dma((2, ny)),
        ],
        compiler_params=pltpu.CompilerParams(
            collective_id=0, has_side_effects=True, vmem_limit_bytes=16 * 1024 * 1024
        ),
    )(state_prev, diffusivity, vapour, cos_zenith, albedo, day_mask, absorb, weight)
    held = [pltpu.with_memory_space_constraint(h, pltpu.VMEM) for h in held]
    out = jax.ShapeDtypeStruct(cells, F32)
    return pl.pallas_call(
        finish_kernel,
        out_shape=(out, out, out),
        in_specs=[vmem] * 11,
        out_specs=(hbm, hbm, hbm),
        scratch_shapes=[
            pltpu.VMEM(cells, F32),
            pltpu.VMEM(cells, F32),
            pltpu.VMEM(cells, F32),
            scales,
            partial,
            dma((3, 4)),
        ],
        compiler_params=pltpu.CompilerParams(vmem_limit_bytes=8 * 1024 * 1024),
    )(*held)


def solution(mesh):
    cells = P("gy", None, "gx")
    columns = P("gy", "gx")
    return jax.shard_map(
        functools.partial(body, (mesh.shape["gx"], mesh.shape["gy"])),
        mesh=mesh,
        in_specs=(cells, cells, cells, columns, columns, P(), P(), P(("gx", "gy"))),
        out_specs=(cells, cells, cells),
        check_vma=False,
    )
```

profile of v0, /device:TPU:0, one launch (start us, length us, event | category | flops | bytes accessed | tf_op | source)
XLA Modules:
  0.0 66.2 jit_solution(8992087251673570325)
XLA Ops:
  0.6 0.0 copy-start
  0.6 1.2 %copy-done = f32[16,128,128]{2,1,0:T(8,128)S(1)} copy-done((f32[16,128,128]{2,1,0:T(8,128)S(1)}, f32[16,128,128]{2,1,0:T(8,128)}, u32[]{:S(2)}) %copy-start) | copy-done | bytes 1048600
  1.9 0.0 copy-start.1
  1.9 1.2 %copy-done.1 = f32[16,128,128]{2,1,0:T(8,128)S(1)} copy-done((f32[16,128,128]{2,1,0:T(8,128)S(1)}, f32[16,128,128]{2,1,0:T(8,128)}, u32[]{:S(2)}) %copy-start.1) | copy-done | bytes 1048600
  3.1 0.0 copy-start.2
  3.1 1.2 %copy-done.2 = f32[16,128,128]{2,1,0:T(8,128)S(1)} copy-done((f32[16,128,128]{2,1,0:T(8,128)S(1)}, f32[16,128,128]{2,1,0:T(8,128)}, u32[]{:S(2)}) %copy-start.2) | copy-done | bytes 1048600
  4.3 0.0 copy-start.3
  4.3 0.8 %copy-done.3 = f32[128,112]{0,1:T(8,128)S(1)} copy-done((f32[128,112]{0,1:T(8,128)S(1)}, f32[128,112]{0,1:T(8,128)}, u32[]{:S(2)}) %copy-start.3) | copy-done | bytes 57368
  5.1 0.0 copy-start.4
  5.1 0.7 %copy-done.4 = f32[16,128]{1,0:T(8,128)S(1)} copy-done((f32[16,128]{1,0:T(8,128)S(1)}, f32[16,128]{1,0:T(8,128)}, u32[]{:S(2)}) %copy-start.4) | copy-done | bytes 8216
  5.8 0.0 copy-start.5
  5.8 0.7 %copy-done.5 = f32[16,128]{1,0:T(8,128)S(1)} copy-done((f32[16,128]{1,0:T(8,128)S(1)}, f32[16,128]{1,0:T(8,128)}, u32[]{:S(2)}) %copy-start.5) | copy-done | bytes 8216
  6.5 0.0 copy-start.6
  6.5 0.7 copy-done.6
  7.2 0.0 copy-start.7
  7.2 0.7 copy-done.7
  7.8 54.4 %shard_map.103 = (f32[6,18,128,128]{3,2,1,0:T(8,128)S(1)}, f32[18,128,128]{2,1,0:T(8,128)S(1)}, f32[18,128,128]{2,1,0:T(8,128)S(1)}, f32[16,128,128]{2,1,0:T(8,1...) custom-call(f32[16,128,128]{2,1,0:T(8,128)S(1)} %copy-done, ...), custom_call_target="tpu_custom_call" | custom-call | tf_op jit(solution)/shard_map/pallas_call | solution.py:539
  62.3 3.9 %shard_map.104 = (f32[16,128,128]{2,1,0:T(8,128)}, f32[16,128,128]{2,1,0:T(8,128)}, f32[16,128,128]{2,1,0:T(8,128)}) custom-call(f32[6,18,128,128]{3,2,1,0:T(8,128)S(1)} %get-tuple-element.14.basis, f32[18,128,128]{2,1,0:T(8,128)S(1)} %get-tuple-element.15.xs, f32[18,128,128]{2,1,0:T(8,128)S(1)} %get-tuple-element.16.ds, ...), custom_call_target="tpu_custom_call" | custom-call | tf_op jit(solution)/shard_map/pallas_call | solution.py:584
Async XLA Ops:
  0.6 1.2 %copy-start = (f32[16,128,128]{2,1,0:T(8,128)S(1)}, f32[16,128,128]{2,1,0:T(8,128)}, u32[]{:S(2)}) copy-start(f32[16,128,128]{2,1,0:T(8,128)} %state_hbm.1) | copy-start | bytes 3145732
  1.9 1.2 %copy-start.1 = (f32[16,128,128]{2,1,0:T(8,128)S(1)}, f32[16,128,128]{2,1,0:T(8,128)}, u32[]{:S(2)}) copy-start(f32[16,128,128]{2,1,0:T(8,128)} %diff_hbm.1) | copy-start | bytes 3145732
  3.1 1.2 %copy-start.2 = (f32[16,128,128]{2,1,0:T(8,128)S(1)}, f32[16,128,128]{2,1,0:T(8,128)}, u32[]{:S(2)}) copy-start(f32[16,128,128]{2,1,0:T(8,128)} %vapour_hbm.1) | copy-start | bytes 3145732
  4.3 0.8 %copy-start.3 = (f32[128,112]{0,1:T(8,128)S(1)}, f32[128,112]{0,1:T(8,128)}, u32[]{:S(2)}) copy-start(f32[128,112]{0,1:T(8,128)} %param.13) | copy-start | bytes 172036
  5.1 0.7 %copy-start.4 = (f32[16,128]{1,0:T(8,128)S(1)}, f32[16,128]{1,0:T(8,128)}, u32[]{:S(2)}) copy-start(f32[16,128]{1,0:T(8,128)} %cos_hbm.1) | copy-start | bytes 24580
  5.8 0.7 %copy-start.5 = (f32[16,128]{1,0:T(8,128)S(1)}, f32[16,128]{1,0:T(8,128)}, u32[]{:S(2)}) copy-start(f32[16,128]{1,0:T(8,128)} %albedo_hbm.1) | copy-start | bytes 24580
  6.5 0.7 copy-start.6
  7.2 0.7 copy-start.7
where the time goes:
time: 66.6 us; the launch traced here: 66.2 us
  Pallas kernels  58.3 us (88%)
  local copies, waits for them, and re-layouts  7.19 us (11%)
    pallas_call x1, Pallas kernels, body(): pl.pallas_call(functools.partial(solve_kernel, nx, ny), out_shape=[pltpu....  54.4 us
    unnamed x16, local copies, waits for them, and re-layouts  7.19 us
    pallas_call x1, Pallas kernels, body(): pl.pallas_call(finish_kernel, out_shape=(out, out, out), in_specs=[vmem]...  3.89 us

commit v1 on v0

--- a/solution.py
+++ b/solution.py
@@ -11,14 +11,16 @@
 ITERS = 5
 SUB = 8
 WINDOWS = ITERS + 3
-UNROLL = 32
+SHARES = (0, 1, 3, 5, 7, 9, 11, 13, 15)
+UNROLL = 64
+GROUP = 4
 LOG2E = math.log2(math.e)
 MESH = pl.DeviceIdType.MESH
 F32 = jnp.float32
 
 
 def edge(rows, w):
-    return max(0, rows * (2 * w - 1) // (2 * WINDOWS))
+    return rows * SHARES[w] // 16
 
 
 def radiate(j, state, vapour_ref, cos_ref, albedo_ref, maskv_ref, wcol_ref, wide, scales, partial, net_ref):
@@ -57,26 +59,25 @@
 def solve_kernel(
     nx, ny,
     state_hbm, diff_hbm, vapour_hbm, cos_hbm, albedo_hbm, mask_hbm, absorb_hbm, weight_hbm,
-    basis, xs, ds, vapour_ref, cos_ref, albedo_ref, net_ref, wide, wcol, maskv, coef,
-    root, degree, gain_d, inverse_d, absorb, weight_row, mask_smem,
-    lon_send, lon_recv, lon_halo, scales, partial, sums, mine, stage_one, half_sum, stage_two,
+    basis, state_ref, ds, vapour_ref, cos_ref, albedo_ref, net_ref, wide, wcol, maskv, coef,
+    xs, diff_ref, root, degree, gain_d, inverse_d, absorb, weight_row, mask_smem,
+    lon_send, lon_recv, lon_root, scales, partial, sums, mine, stage_one, half_sum, stage_two,
     in_sem, lat_ssem, lat_rsem, lon_ssem, lon_rsem, one_ssem, one_rsem, two_ssem, two_rsem,
 ):
     rows, levels, lanes = vapour_ref.shape
     gpoints = wide.shape[1]
-    tiles = levels // SUB
-    per = lanes // (2 * tiles)
+    tiles = lanes // SUB
+    per = GROUP
     groups = rows // per
     moments = 2 * ITERS + 1
     ix = lax.axis_index("gx")
     iy = lax.axis_index("gy")
     gx_east, gx_west = lax.rem(ix + 1, nx), lax.rem(ix + nx - 1, nx)
-    inside = pl.ds(1, rows)
 
     loads = [
         pltpu.make_async_copy(src, dst, in_sem.at[i])
         for i, (src, dst) in enumerate([
-            (diff_hbm, ds.at[inside]), (state_hbm, xs.at[inside]), (absorb_hbm, absorb),
+            (diff_hbm, diff_ref), (state_hbm, state_ref), (absorb_hbm, absorb),
             (weight_hbm, weight_row), (mask_hbm, mask_smem), (cos_hbm, cos_ref),
             (albedo_hbm, albedo_ref), (vapour_hbm, vapour_ref),
         ])
@@ -94,12 +95,11 @@
             barrier, inc=1, device_id=(ix, lax.rem(iy + d, ny)), device_id_type=MESH
         )
 
-    lane = lax.broadcasted_iota(jnp.int32, (SUB, lanes), 1)
-    sub = lax.broadcasted_iota(jnp.int32, (SUB, lanes), 0)
-    first_lane, last_lane = lane == 0, lane == lanes - 1
+    lane = lax.broadcasted_iota(jnp.int32, (SUB, levels), 1)
+    sub = lax.broadcasted_iota(jnp.int32, (SUB, levels), 0)
+    first_lane, last_lane = lane == 0, lane == levels - 1
     first_sub, last_sub = sub == 0, sub == SUB - 1
-    even_lane = (lane & 1) == 0
-    zero = jnp.zeros((SUB, lanes), F32)
+    zero = jnp.zeros((SUB, levels), F32)
 
     def field(k):
         return ds if k == 0 else xs if k == 1 else basis.at[k - 2]
@@ -117,7 +117,7 @@
 
     def lon_copy(k, side):
         return pltpu.make_async_remote_copy(
-            src_ref=lon_send.at[k],
+            src_ref=lon_send.at[k, side],
             dst_ref=lon_recv.at[k, side],
             send_sem=lon_ssem.at[k, side],
             recv_sem=lon_rsem.at[k, side],
@@ -151,38 +151,28 @@
         for side in range(2):
             lon_copy(k, side).wait()
 
-    def merged(k, g):
-        west = lon_recv[k, 1, g * SUB:(g + 1) * SUB, :]
-        east = pltpu.roll(lon_recv[k, 0, g * SUB:(g + 1) * SUB, :], lanes - 2, 1)
-        return jnp.where(even_lane, west, east)
-
-    bits = [((lane >> (1 + b)) & 1) == 1 for b in range((lanes // 2 - 1).bit_length())]
-
-    def pack(pieces):
-        level = [pltpu.roll(piece, (2 * q + 1) % lanes, 1) for q, piece in enumerate(pieces)]
-        for mask in bits:
-            level = [jnp.where(mask, b, a) for a, b in zip(level[::2], level[1::2])]
-        return level[0]
-
-    def group_rows(g):
-        return pl.ds(pl.multiple_of(g * SUB, SUB), SUB)
-
-    def lon_pair(value, halo, q):
-        moved = pltpu.roll(halo, (lanes - 2 * q) % lanes, 1)
+    def edges(k, j, values):
+        lon_send[k, 0, pl.ds(j, 1), :] = values[0][0:1, :]
+        lon_send[k, 1, pl.ds(j, 1), :] = values[-1][-1:, :]
+
+    def level_pair(value):
         return (
-            jnp.where(last_lane, moved, pltpu.roll(value, lanes - 1, 1)),
-            jnp.where(first_lane, moved, pltpu.roll(value, 1, 1)),
-        )
-
-    def vertical_pair(values):
+            jnp.where(last_lane, 0.0, pltpu.roll(value, levels - 1, 1)),
+            jnp.where(first_lane, 0.0, pltpu.roll(value, 1, 1)),
+        )
+
+    def lon_pair(values, halo, j):
         later = [pltpu.roll(v, 1, 0) for v in values]
         sooner = [pltpu.roll(v, SUB - 1, 0) for v in values]
-        above = [jnp.where(first_sub, later[t - 1] if t else zero, later[t]) for t in range(tiles)]
-        below = [
-            jnp.where(last_sub, sooner[t + 1] if t < tiles - 1 else zero, sooner[t])
+        west, east = halo[1, pl.ds(j, 1), :], halo[0, pl.ds(j, 1), :]
+        at_west = [
+            jnp.where(first_sub, later[t - 1] if t else west, later[t]) for t in range(tiles)
+        ]
+        at_east = [
+            jnp.where(last_sub, sooner[t + 1] if t < tiles - 1 else east, sooner[t])
             for t in range(tiles)
         ]
-        return above, below
+        return at_west, at_east
 
     def plane_of(ref, j):
         return [ref[j, t * SUB:(t + 1) * SUB, :] for t in range(tiles)]
@@ -220,41 +210,38 @@
         return total
 
     def all_lanes(values):
-        shift = lanes // 2
-        while shift:
-            values = values + pltpu.roll(values, shift, 1)
-            shift //= 2
-        return values
+        return jnp.broadcast_to(jnp.sum(values, 1, keepdims=True), values.shape)
 
     def window(first, last):
         @pl.loop(first, last)
         def _(j):
             radiate(
-                j, xs[j + 1], vapour_ref, cos_ref, albedo_ref, maskv, wcol, wide, scales,
+                j, state_ref[j], vapour_ref, cos_ref, albedo_ref, maskv, wcol, wide, scales,
                 partial, net_ref,
             )
 
     for k in range(2, 2 + ITERS):
         @pl.when(iy == 0)
         def _():
-            basis[k - 2, 0] = jnp.zeros((levels, lanes), F32)
+            basis[k - 2, 0] = jnp.zeros((lanes, levels), F32)
 
         @pl.when(iy == ny - 1)
         def _():
-            basis[k - 2, rows + 1] = jnp.zeros((levels, lanes), F32)
+            basis[k - 2, rows + 1] = jnp.zeros((lanes, levels), F32)
 
     for k in range(2):
         loads[k].wait()
-        if k == 0:
-            pl.semaphore_wait(barrier, nx + ny - 2)
-
-        @pl.loop(0, groups)
-        def _(g):
-            pieces = []
-            for i in range(per):
-                pieces += plane_of(field(k), g * per + i + 1)
-            lon_send[k, group_rows(g), :] = pack(pieces)
-
+
+        given = diff_ref if k == 0 else state_ref
+
+        @pl.loop(0, rows, unroll=4)
+        def _(j):
+            turned = given[j].T
+            field(k)[j + 1] = turned
+            edges(k, j, [turned])
+
+    pl.semaphore_wait(barrier, nx + ny - 2)
+    for k in range(2):
         send_halo(k)
 
     def spread(j, total):
@@ -303,8 +290,8 @@
 
     @pl.when(iy == 0)
     def _():
-        root[0] = jnp.zeros((levels, lanes), F32)
-        xs[0] = jnp.zeros((levels, lanes), F32)
+        root[0] = jnp.zeros((lanes, levels), F32)
+        xs[0] = jnp.zeros((lanes, levels), F32)
 
     @pl.when(iy < ny - 1)
     def _():
@@ -312,32 +299,28 @@
 
     @pl.when(iy == ny - 1)
     def _():
-        root[rows + 1] = jnp.zeros((levels, lanes), F32)
-        xs[rows + 1] = jnp.zeros((levels, lanes), F32)
-
-    for g in range(groups):
-        d = merged(0, g)
-        lon_halo[0, g * SUB:(g + 1) * SUB, :] = d * lax.rsqrt(d)
-        lon_halo[1, g * SUB:(g + 1) * SUB, :] = merged(1, g)
+        root[rows + 1] = jnp.zeros((lanes, levels), F32)
+        xs[rows + 1] = jnp.zeros((lanes, levels), F32)
+
+    for side in range(2):
+        d = lon_recv[0, side]
+        lon_root[side] = d * lax.rsqrt(d)
 
     @pl.loop(0, groups)
     def _(g):
-        root_halo = lon_halo[0, group_rows(g), :]
-        x_halo = lon_halo[1, group_rows(g), :]
-        pieces = []
         for i in range(per):
             j = g * per + i
             s_here, x_here = plane_of(root, j + 1), plane_of(xs, j + 1)
-            s_above, s_below = vertical_pair(s_here)
-            x_above, x_below = vertical_pair(x_here)
+            s_west, s_east = lon_pair(s_here, lon_root, j)
+            x_west, x_east = lon_pair(x_here, lon_recv.at[1], j)
+            started = []
             for t in range(tiles):
                 at = pl.ds(t * SUB, SUB)
-                q = i * tiles + t
-                s_pairs = lon_pair(s_here[t], root_halo, q) + (
-                    root[j + 2, at, :], root[j, at, :], s_above[t], s_below[t]
+                s_pairs = level_pair(s_here[t]) + (
+                    root[j + 2, at, :], root[j, at, :], s_west[t], s_east[t]
                 )
-                x_pairs = lon_pair(x_here[t], x_halo, q) + (
-                    xs[j + 2, at, :], xs[j, at, :], x_above[t], x_below[t]
+                x_pairs = level_pair(x_here[t]) + (
+                    xs[j + 2, at, :], xs[j, at, :], x_west[t], x_east[t]
                 )
                 around, change = None, None
                 for s, x in zip(s_pairs, x_pairs):
@@ -347,8 +330,8 @@
                 degree[j, at, :] = s_here[t] * around
                 start = ds[j + 1, at, :] * change
                 basis[0, j + 1, at, :] = start
-                pieces.append(start)
-        lon_send[2, group_rows(g), :] = pack(pieces)
+                started.append(start)
+            edges(2, j, started)
 
     send_halo(2)
     window(edge(rows, 1), edge(rows, 2))
@@ -356,26 +339,24 @@
     count = nx * ny * rows * levels * lanes
     squares = all_lanes(jnp.sum(squares, 0, keepdims=True))
     half = 6.0 * jnp.exp(jnp.log(squares * (1.0 / count)) * (1.0 / 6.0))
-    twice = jnp.broadcast_to(2.0 / half, (SUB, lanes))
+    twice = jnp.broadcast_to(2.0 / half, (SUB, levels))
 
     def advance(k, first, last):
         wait_halo(2 + k)
-        for g in range(groups):
-            lon_halo[0, g * SUB:(g + 1) * SUB, :] = merged(2 + k, g)
+        halo = lon_recv.at[2 + k]
         here, there = basis.at[k], basis.at[k + 1]
 
         def step(g, totals):
-            halo = lon_halo[0, group_rows(g), :]
-            pieces = []
             parts = [zero] * len(totals)
             for i in range(per):
                 j = g * per + i
                 u = plane_of(here, j + 1)
-                above, below = vertical_pair(u)
+                west, east = lon_pair(u, halo, j)
+                latest = []
                 for t in range(tiles):
                     at = pl.ds(t * SUB, SUB)
-                    east, west = lon_pair(u[t], halo, i * tiles + t)
-                    around = ((east + west) + (above[t] + below[t])) + (
+                    below, above = level_pair(u[t])
+                    around = ((east[t] + west[t]) + (above + below)) + (
                         here[j + 2, at, :] + here[j, at, :]
                     )
                     if first:
@@ -393,9 +374,9 @@
                     parts[1] = parts[1] + weighed * later
                     if first:
                         parts[2] = parts[2] + (u[t] * inverse_d[j, at, :]) * u[t]
-                    pieces.append(later)
-            if not last:
-                lon_send[3 + k, group_rows(g), :] = pack(pieces)
+                    latest.append(later)
+                if not last:
+                    edges(3 + k, j, latest)
             return tuple(a + b for a, b in zip(totals, parts))
 
         totals = lax.fori_loop(0, groups, step, (zero,) * (3 if first else 2))
@@ -471,37 +452,32 @@
 
 
 def finish_kernel(
-    basis, xs, ds, vapour_ref, cos_ref, albedo_ref, net_ref, wide, wcol, maskv, coef,
+    basis, state_ref, ds, vapour_ref, cos_ref, albedo_ref, net_ref, wide, wcol, maskv, coef,
     next_hbm, residual_hbm, net_hbm,
     next_ref, residual_ref, rest, scales, partial, sems,
 ):
-    rows, levels, lanes = vapour_ref.shape
-    tiles = levels // SUB
+    rows = vapour_ref.shape[0]
     done = edge(rows, WINDOWS)
     chunk = rows // 4
     early = pltpu.make_async_copy(
         net_ref.at[pl.ds(0, done)], net_hbm.at[pl.ds(0, done)], sems.at[0, 0]
     )
     early.start()
-    lines = [
-        jnp.broadcast_to(coef[m:m + 1, :], (SUB, lanes)) for m in range(2 * ITERS + 1)
-    ]
+    lines = [coef[m:m + 1, :] for m in range(2 * ITERS + 1)]
     gain, res = lines[:ITERS], lines[ITERS:]
     copies = []
     for c in range(rows // chunk):
-        @pl.loop(c * chunk, (c + 1) * chunk)
+        @pl.loop(c * chunk, (c + 1) * chunk, unroll=chunk)
         def _(j):
-            for t in range(tiles):
-                at = pl.ds(t * SUB, SUB)
-                base = [basis[k, j + 1, at, :] for k in range(ITERS + 1)]
-                scale = lax.rsqrt(ds[j + 1, at, :])
-                moved, left = gain[0] * base[0], res[0] * base[0]
-                for k in range(1, ITERS + 1):
-                    if k < ITERS:
-                        moved = moved + gain[k] * base[k]
-                    left = left + res[k] * base[k]
-                next_ref[j, at, :] = xs[j + 1, at, :] + scale * moved
-                residual_ref[j, at, :] = scale * left
+            base = [basis[k, j + 1] for k in range(ITERS + 1)]
+            scale = lax.rsqrt(ds[j + 1])
+            moved, left = gain[0] * base[0], res[0] * base[0]
+            for k in range(1, ITERS + 1):
+                if k < ITERS:
+                    moved = moved + gain[k] * base[k]
+                left = left + res[k] * base[k]
+            next_ref[j] = state_ref[j] + (scale * moved).T
+            residual_ref[j] = (scale * left).T
 
         part = pl.ds(c * chunk, chunk)
         for i, (source, target) in enumerate([(next_ref, next_hbm), (residual_ref, residual_hbm)]):
@@ -510,7 +486,7 @@
 
     for j in range(done, rows):
         radiate(
-            j, xs[j + 1], vapour_ref, cos_ref, albedo_ref, maskv, wcol, wide, scales,
+            j, state_ref[j], vapour_ref, cos_ref, albedo_ref, maskv, wcol, wide, scales,
             partial, rest,
         )
     late = pltpu.make_async_copy(
@@ -531,16 +507,16 @@
     hbm = pl.BlockSpec(memory_space=pltpu.HBM)
     dma = pltpu.SemaphoreType.DMA
     kinds = ITERS + 2
-    packs = 2 * rows * (levels // SUB) // lanes * SUB
     cells = (rows, levels, lanes)
-    around = (rows + 2, levels, lanes)
+    turned = (rows, lanes, levels)
+    around = (rows + 2, lanes, levels)
     scales = pltpu.VMEM((2, levels, lanes), F32)
     partial = pltpu.VMEM((levels * SUB, lanes), F32)
     held = pl.pallas_call(
         functools.partial(solve_kernel, nx, ny),
         out_shape=[
             pltpu.VMEM((ITERS + 1,) + around, F32),
-            pltpu.VMEM(around, F32),
+            pltpu.VMEM(cells, F32),
             pltpu.VMEM(around, F32),
             pltpu.VMEM(cells, F32),
             pltpu.VMEM((rows, lanes), F32),
@@ -549,36 +525,41 @@
             pltpu.VMEM((levels, gpoints, lanes), F32),
             pltpu.VMEM((gpoints, lanes), F32),
             pltpu.VMEM((rows, lanes), F32),
-            pltpu.VMEM((2 * SUB, lanes), F32),
+            pltpu.VMEM((2 * SUB, levels), F32),
         ],
         in_specs=[hbm] * 8,
         out_specs=[vmem] * 11,
         scratch_shapes=[
             pltpu.VMEM(around, F32),
             pltpu.VMEM(cells, F32),
-            pltpu.VMEM(cells, F32),
-            pltpu.VMEM(cells, F32),
+            pltpu.VMEM(around, F32),
+            pltpu.VMEM(turned, F32),
+            pltpu.VMEM(turned, F32),
+            pltpu.VMEM(turned, F32),
             pltpu.VMEM((gpoints, levels), F32),
             pltpu.VMEM((1, gpoints), F32),
             pltpu.SMEM((rows,), jnp.int32),
-            pltpu.VMEM((kinds, packs, lanes), F32),
-            pltpu.VMEM((kinds, 2, packs, lanes), F32),
-            pltpu.VMEM((2, packs, lanes), F32),
+            pltpu.VMEM((kinds, 2, rows, levels), F32),
+            pltpu.VMEM((kinds, 2, rows, levels), F32),
+            pltpu.VMEM((2, rows, levels), F32),
             scales,
             partial,
-            pltpu.VMEM((2 * ITERS + 1, SUB, lanes), F32),
-            pltpu.VMEM((2, 2 * SUB, lanes), F32),
-            pltpu.VMEM((2, nx, 2 * SUB, lanes), F32),
-            pltpu.VMEM((2, 2 * SUB, lanes), F32),
-            pltpu.VMEM((2, ny, 2 * SUB, lanes), F32),
+            pltpu.VMEM((2 * ITERS + 1, SUB, levels), F32),
+            pltpu.VMEM((2, 2 * SUB, levels), F32),
+            pltpu.VMEM((2, nx, 2 * SUB, levels), F32),
+            pltpu.VMEM((2, 2 * SUB, levels), F32),
+            pltpu.VMEM((2, ny, 2 * SUB, levels), F32),
             dma((8,)),
             dma((kinds, 2)), dma((kinds, 2)), dma((kinds, 2)), dma((kinds, 2)),
             dma((2, nx)), dma((2, nx)), dma((2, ny)), dma((2, ny)),
         ],
         compiler_params=pltpu.CompilerParams(
-            collective_id=0, has_side_effects=True, vmem_limit_bytes=16 * 1024 * 1024
+            collective_id=0, has_side_effects=True, vmem_limit_bytes=18 * 1024 * 1024
         ),
-    )(state_prev, diffusivity, vapour, cos_zenith, albedo, day_mask, absorb, weight)
+    )(*[
+        pltpu.with_memory_space_constraint(a, pltpu.HBM)
+        for a in (state_prev, diffusivity, vapour, cos_zenith, albedo, day_mask, absorb, weight)
+    ])
     held = [pltpu.with_memory_space_constraint(h, pltpu.VMEM) for h in held]
     out = jax.ShapeDtypeStruct(cells, F32)
     return pl.pallas_call(

time: 66.6 us -> 53.2 us (0.80)
  local copies, waits for them, and re-layouts: 7.19 us -> 0 us
  Pallas kernels: 58.3 us -> 52.4 us
    unnamed x16 -> x0, local copies, waits for them, and re-layouts: 7.19 us -> none
    pallas_call x1, Pallas kernels: 54.4 us -> 48.7 us  [body(): pl.pallas_call(functools.partial(solve_kernel, nx, ny), out_shape=[pltpu....]
where the time goes in v1:
time: 53.2 us; the launch traced here: 53 us
  Pallas kernels  52.4 us (98%)
  between operations  0.64 us (1%)
    pallas_call x1, Pallas kernels, body(): pl.pallas_call(functools.partial(solve_kernel, nx, ny), out_shape=[pltpu....  48.7 us
    pallas_call x1, Pallas kernels, body(): pl.pallas_call(finish_kernel, out_shape=(out, out, out), in_specs=[vmem]...  3.7 us

profile of v1, /device:TPU:0, one launch (start us, length us, event | category | flops | bytes accessed | tf_op | source)
XLA Modules:
  0.0 53.0 jit_solution(15449409637470813624)
XLA Ops:
  0.6 48.7 %shard_map.103 = (f32[6,18,128,128]{3,2,1,0:T(8,128)S(1)}, f32[16,128,128]{2,1,0:T(8,128)S(1)}, f32[18,128,128]{2,1,0:T(8,128)S(1)}, f32[16,128,128]{2,1,0:T(8,1...) custom-call(f32[16,128,128]{2,1,0:T(8,128)} %state_hbm.1, ...), custom_call_target="tpu_custom_call" | custom-call | tf_op jit(solution)/shard_map/pallas_call | solution.py:515
  49.3 3.7 %shard_map.104 = (f32[16,128,128]{2,1,0:T(8,128)}, f32[16,128,128]{2,1,0:T(8,128)}, f32[16,128,128]{2,1,0:T(8,128)}) custom-call(f32[6,18,128,128]{3,2,1,0:T(8,128)S(1)} %get-tuple-element.14.basis, f32[16,128,128]{2,1,0:T(8,128)S(1)} %get-tuple-element.15.state_ref, f32[18,128,128]{2,1,0:T(8,128)S(1)} %get-tuple-element.16.ds, ...), custom_call_target="tpu_custom_call" | custom-call | tf_op jit(solution)/shard_map/pallas_call | solution.py:565

commit v2 on v1

--- a/solution.py
+++ b/solution.py
@@ -229,34 +229,31 @@
         def _():
             basis[k - 2, rows + 1] = jnp.zeros((lanes, levels), F32)
 
-    for k in range(2):
-        loads[k].wait()
-
-        given = diff_ref if k == 0 else state_ref
-
-        @pl.loop(0, rows, unroll=4)
-        def _(j):
-            turned = given[j].T
-            field(k)[j + 1] = turned
-            edges(k, j, [turned])
+    loads[0].wait()
+
+    def spread(j, total):
+        turned = diff_ref[j].T
+        ds[j + 1] = turned
+        edges(0, j, [turned])
+        reciprocal = lax.rsqrt(turned)
+        root[j + 1] = turned * reciprocal
+        inverse_d[j] = reciprocal * reciprocal
+        square = turned * turned
+        return total + jnp.sum((square * square * square).reshape(tiles, SUB, levels), 0)
+
+    squares = lax.fori_loop(0, rows, spread, zero, unroll=4)
+    loads[1].wait()
+
+    @pl.loop(0, rows, unroll=4)
+    def _(j):
+        turned = state_ref[j].T
+        xs[j + 1] = turned
+        edges(1, j, [turned])
 
     pl.semaphore_wait(barrier, nx + ny - 2)
     for k in range(2):
         send_halo(k)
 
-    def spread(j, total):
-        part = zero
-        for t in range(tiles):
-            here = pl.ds(t * SUB, SUB)
-            d = ds[j + 1, here, :]
-            reciprocal = lax.rsqrt(d)
-            root[j + 1, here, :] = d * reciprocal
-            inverse_d[j, here, :] = reciprocal * reciprocal
-            square = d * d
-            part = part + square * square * square
-        return total + part
-
-    squares = lax.fori_loop(0, rows, spread, zero)
     mine[0] = jnp.concatenate([squares, jnp.zeros_like(squares)], 0)
     reduce_start(0, 0)
 
@@ -399,7 +396,7 @@
     half_sum[1] = reduce_end(1, 0)
     reduce_start(1, 1)
     window(edge(rows, ITERS + 2), edge(rows, ITERS + 3))
-    values = all_lanes(reduce_end(1, 1))
+    values = reduce_end(1, 1)
     raw = [values[m:m + 1, :] for m in range(moments)]
 
     mu = [raw[0], raw[1]]
@@ -421,7 +418,7 @@
                 terms[i] + terms[i + 1] if i + 1 < len(terms) else terms[i]
                 for i in range(0, len(terms), 2)
             ]
-        return terms[0]
+        return all_lanes(terms[0])
 
     centre = half + 1.0
     one = jnp.ones_like(half)

time: 53.2 us -> 53.3 us (level)
  no operation moved by 1% of the time
where the time goes in v2:
time: 53.3 us; the launch traced here: 53.2 us
  Pallas kernels  52.5 us (98%)
  between operations  0.64 us (1%)
    pallas_call x1, Pallas kernels, body(): pl.pallas_call(functools.partial(solve_kernel, nx, ny), out_shape=[pltpu....  48.8 us
    pallas_call x1, Pallas kernels, body(): pl.pallas_call(finish_kernel, out_shape=(out, out, out), in_specs=[vmem]...  3.7 us

profile of v2, /device:TPU:0, one launch (start us, length us, event | category | flops | bytes accessed | tf_op | source)
XLA Modules:
  0.0 53.2 jit_solution(14816292292803132634)
XLA Ops:
  0.6 48.8 %shard_map.103 = (f32[6,18,128,128]{3,2,1,0:T(8,128)S(1)}, f32[16,128,128]{2,1,0:T(8,128)S(1)}, f32[18,128,128]{2,1,0:T(8,128)S(1)}, f32[16,128,128]{2,1,0:T(8,1...) custom-call(f32[16,128,128]{2,1,0:T(8,128)} %state_hbm.1, ...), custom_call_target="tpu_custom_call" | custom-call | tf_op jit(solution)/shard_map/pallas_call | solution.py:512
  49.5 3.7 %shard_map.104 = (f32[16,128,128]{2,1,0:T(8,128)}, f32[16,128,128]{2,1,0:T(8,128)}, f32[16,128,128]{2,1,0:T(8,128)}) custom-call(f32[6,18,128,128]{3,2,1,0:T(8,128)S(1)} %get-tuple-element.14.basis, f32[16,128,128]{2,1,0:T(8,128)S(1)} %get-tuple-element.15.state_ref, f32[18,128,128]{2,1,0:T(8,128)S(1)} %get-tuple-element.16.ds, ...), custom_call_target="tpu_custom_call" | custom-call | tf_op jit(solution)/shard_map/pallas_call | solution.py:562
